TPU v7x, 512 devices: a whole 4x8x8 slice. The times are simulated.
512 devices in a mesh: section: 8 (over z_hi, core), dp: 64 (over y, x, z_lo).
Axes of the slice: x: 4, y: 8, z: 8 (z_hi: 4, z_lo: 2; z = z_hi * 2 + z_lo), core: 2. Of those that a mesh axis runs over, the one named last changes fastest.
Arguments:
- tokens: bfloat16 [2, 64, 80, 1024], P(None, 'dp'), may hold values from -6 to 6
- w_qkv: bfloat16 [8, 1024, 1536], P('section', 'dp'), may hold values from -0.1875 to 0.1875
- w_output: bfloat16 [8, 512, 1024], P('section', None, 'dp'), may hold values from -0.25 to 0.25
- tangent_value: bfloat16 [8, 2, 1024, 512], P('section', None, 'dp'), may hold values from -0.1875 to 0.1875
- tangent_output: bfloat16 [8, 2, 512, 1024], P('section', None, None, 'dp'), may hold values from -0.25 to 0.25
- layer_gain: float32 [8, 1024], P('section'), may hold values from 0.5 to 1.5
- final_gain: float32 [1024], replicated, may hold values from 0.5 to 1.5
- head: bfloat16 [1024, 1000], P(None, 'section'), may hold values from -0.1875 to 0.1875
Outputs:
- mean_logits: float32 [2, 64, 1000], P(None, 'dp', 'section')
- variance: float32 [2, 64, 1000], P(None, 'dp', 'section')
All inputs are finite; a program needn't handle non-finite values.
Results may differ from a plain program's by a relative error of at most 0.018.
Values may be sent and summed in bfloat16 or wider, within the bound.
No kernel may reach another device: no remote copies, remote signals or barrier semaphores. Data moves between devices by JAX's collectives and lax.ppermute only.
A program may use at most 64 MiB of HBM per device.

v0:
```python
import jax
import jax.numpy as jnp
from jax import lax
from jax.sharding import PartitionSpec as P

HEADS = 8
HEAD = 64
TANGENTS = 2
HD = 512
epsilon = 1e-06


def gather_turned(arrays, axis, dims):
    turned = [jnp.moveaxis(a, dim, 0) for a, dim in zip(arrays, dims)]
    both = jnp.concatenate([t.reshape(len(t), -1) for t in turned], axis=1)
    result, at, gathered = (lax.all_gather(both, axis, axis=0, tiled=True), 0, [])
    for t, dim in zip(turned, dims):
        share = result[:, at : at + t[0].size].reshape(-1, *t.shape[1:])
        gathered.append(jnp.moveaxis(share, 0, dim))
        at += t[0].size
    return tuple(gathered)


def passed_along(block, axis, distance):
    devices = range(lax.axis_size(axis))
    route = [(i - distance, i) for i in devices if i - distance in devices]
    return lax.ppermute(block, axis, route)


def picked(shard, axis, root):
    return lax.dynamic_index_in_dim(lax.all_gather(shard, axis), root, 0, keepdims=False)


def contract(spec, left, right):
    return jnp.einsum(spec, left, right, preferred_element_type=jnp.float32)


def norm_jvp(primal, tangents, gains):
    average = jnp.mean(primal, -1, keepdims=True)
    centred = primal - average
    inverse = lax.rsqrt(jnp.mean(centred * centred, -1, keepdims=True) + epsilon)
    dcentred = tangents - jnp.mean(tangents, -1, keepdims=True)
    dinverse = -(inverse**3) * jnp.mean(centred * dcentred, -1, keepdims=True)
    return (centred * inverse * gains, (dcentred * inverse + centred * dinverse) * gains)


def layer_step(state, qkv_weight, out_weight, value_tangent, out_tangent, gains):
    resid = state.astype(jnp.float32)
    normed_zero, normed_rest = norm_jvp(resid[0], resid[1:], gains)
    normed = jnp.concatenate([normed_zero[None], normed_rest]).astype(jnp.bfloat16)
    streams, batch, tokens_here, width = normed.shape
    projected = contract("sbtd,de->sbte", normed, qkv_weight)
    extra_value = contract("btd,kde->kbte", normed[0], value_tangent)
    queries = projected[..., :HD]
    key_rows = projected[..., HD : 2 * HD]
    values = projected[..., 2 * HD :]
    values = jnp.concatenate([values[:1], values[1:] + extra_value])
    shape_heads = (streams, batch, tokens_here, HEADS, HEAD)
    queries = queries.astype(jnp.bfloat16).reshape(shape_heads)
    key_rows = key_rows.astype(jnp.bfloat16).reshape(shape_heads)
    values = values.astype(jnp.bfloat16).reshape(shape_heads)
    factor = HEAD ** (-0.5)
    scores = contract("bqhe,bkhe->bhqk", queries[0], key_rows[0]) * factor
    probs = jax.nn.softmax(scores, -1)
    dscores = (
        contract("sbqhe,bkhe->sbhqk", queries[1:], key_rows[0])
        + contract("bqhe,sbkhe->sbhqk", queries[0], key_rows[1:])
    ) * factor
    dprobs = probs * (dscores - jnp.sum(probs * dscores, -1, keepdims=True))
    probs_low = probs.astype(jnp.bfloat16)
    dprobs_low = dprobs.astype(jnp.bfloat16)
    attended_zero = contract("bhqk,bkhe->bqhe", probs_low, values[0])
    attended_rest = contract("sbhqk,bkhe->sbqhe", dprobs_low, values[0]) + contract(
        "bhqk,sbkhe->sbqhe", probs_low, values[1:]
    )
    attended = jnp.concatenate([attended_zero[None], attended_rest]).astype(jnp.bfloat16)
    attended = attended.reshape(streams, batch, tokens_here, HD)
    output = contract("sbte,ed->sbtd", attended, out_weight)
    extra_out = contract("bte,ked->kbtd", attended[0], out_tangent)
    output = jnp.concatenate([output[:1], output[1:] + extra_out])
    return (resid + output).astype(jnp.bfloat16)


def shards(tokens, w_qkv, w_output, tangent_value, tangent_output, layer_gain, final_gain, head):
    full_qkv, full_output, full_value_tan, full_output_tan = gather_turned(
        (w_qkv, w_output, tangent_value, tangent_output), "dp", (1, 2, 2, 3)
    )
    section_gain = layer_gain[0]

    def advance_layer(state):
        return layer_step(
            state, full_qkv[0], full_output[0], full_value_tan[0], full_output_tan[0], section_gain
        )

    def blank_layer(state):
        return jnp.zeros_like(state)

    section_index = lax.axis_index("section")
    section_count = lax.axis_size("section")
    micro_count = tokens.shape[0]
    image_tokens = tokens.shape[2]
    model_width = tokens.shape[3]
    streams = TANGENTS + 1
    flat_tokens = tokens.reshape(micro_count, image_tokens, model_width)

    def advance(step, carried):
        outgoing, collected = carried
        incoming = passed_along(outgoing, "section", 1)
        source_pick = jnp.clip(step, 0, micro_count - 1)
        source_rows = lax.dynamic_index_in_dim(flat_tokens, source_pick, 0, keepdims=True)
        entering = jnp.concatenate(
            [source_rows[None], jnp.zeros((TANGENTS, 1, image_tokens, model_width), jnp.bfloat16)]
        )
        source = jnp.where(section_index == 0, entering, incoming)
        micro_slot = step - section_index
        active = (micro_slot >= 0) & (micro_slot < micro_count)
        result = lax.cond(active, advance_layer, blank_layer, source)
        store_here = active & (section_index == section_count - 1)
        slot_clip = jnp.clip(micro_slot, 0, micro_count - 1)
        current = lax.dynamic_index_in_dim(collected, slot_clip, 1, keepdims=True)
        update = jnp.where(store_here, result[:, :, 0, :], current)
        collected = lax.dynamic_update_slice_in_dim(collected, update, slot_clip, 1)
        return (result, collected)

    initial = (
        jnp.zeros((streams, 1, image_tokens, model_width), jnp.bfloat16),
        jnp.zeros((streams, micro_count, model_width), jnp.bfloat16),
    )
    ignored, collected = lax.fori_loop(0, section_count + micro_count - 1, advance, initial)
    features = picked(collected, "section", section_count - 1)
    widened = features.astype(jnp.float32)
    final_zero, final_rest = norm_jvp(widened[0], widened[1:], final_gain)
    normed_final = jnp.concatenate([final_zero[None], final_rest]).astype(jnp.bfloat16)
    logits = contract("sbd,dc->sbc", normed_final, head)
    mean_logits = logits[0][:, None, :]
    variance = jnp.sum(logits[1:] * logits[1:], 0)[:, None, :]
    return (mean_logits, variance)


def solution(mesh):
    return jax.shard_map(
        shards,
        mesh=mesh,
        in_specs=(
            P(None, "dp", None, None),
            P("section", "dp", None),
            P("section", None, "dp"),
            P("section", None, "dp", None),
            P("section", None, None, "dp"),
            P("section", None),
            P(),
            P(None, "section"),
        ),
        out_specs=(P(None, "dp", "section"), P(None, "dp", "section")),
        check_vma=False,
    )
```

profile of v0, /device:TPU:5, one launch (start us, length us, event | category | flops | bytes accessed | tf_op | source)
XLA Modules:
  0.0 661.8 jit_solution(5009150919877096323)
XLA Ops:
  10.4 271.7 %all-gather.3.cloned.1.call-done = bf16[1024,4096]{1,0:T(8,128)(2,1)} async-done(((bf16[16,4096]{1,0:T(8,128)(2,1)}), bf16[1024,4096]{1,0:T(8,128)(2,1)}) %all-gather.3.cloned.1.call-update) | async-done | bytes 8388624 | tf_op jit(solution)/shard_map/all_gather | solution.py:16
  282.1 4.6 fusion.96
  291.8 4.0 copy.92
  303.7 272.0 %while.16 = (s32[]{:T(128)}, bf16[3,1,80,1024]{3,2,0,1:T(8,128)(2,1)}, bf16[3,2,1024]{2,0,1:T(4,128)(2,1)}, s32[]{:T(128)}, pred[]{:T(512)}, /*index=5*/bf16[2,8...) while((s32[]{:T(128)}, ...), condition=%wide.region_10.11_spmd, body=%wide.region_0.10_spmd.sunk | while | flops 1414402304 | bytes 55991232 | solution.py:129
  303.7 47.9 %collective-permute-start = (bf16[3,1,80,1024]{3,2,0,1:T(8,128)(2,1)}, bf16[3,1,80,1024]{3,2,0,1:T(8,128)(2,1)S(1)}, u32[]{:S(2)}, u32[]{:S(2)}) collective-permute-start(bf16[3,1,80,1024]{3,2,0,1:T(8,128)(2,1)} %get-tuple-element.501), channel_id=1, source_target_pairs={{0,64},{64,128},{128,192},{192,256},{256,320},{320,384},{384,448},... | collective-permute-start | bytes 1474568 | tf_op jit(solution)/shard_map/while/body/eval_jaxpr/ppermute | solution.py:27
  351.6 6.0 collective-permute-done
  360.4 5.2 collective-permute-start
  365.6 12.1 %collective-permute-done = bf16[3,1,80,1024]{3,2,0,1:T(8,128)(2,1)S(1)} collective-permute-done((bf16[3,1,80,1024]{3,2,0,1:T(8,128)(2,1)}, bf16[3,1,80,1024]{3,2,0,1:T(8,128)(2,1)S(1)}, u32[]{:S(2)}, u32[]{:S(2)}) %collective-permute-start) | collective-permute-done | bytes 491552 | tf_op jit(solution)/shard_map/while/body/eval_jaxpr/ppermute | solution.py:27
  377.7 23.2 %conditional.2 = (bf16[3,1,80,1024]{3,2,0,1:T(8,128)(2,1)}, bf16[3,1,1024]{2,0,1:T(4,128)(2,1)}) conditional(s32[]{:T(128)} %convert_element_type.96, () %tuple.75, (pred[]{:T(512)}, s32[]{:T(128)}, bf16[2,80,1024]{2,1,0:T(8,128)(2,1)}, bf16[3,1,80,1024]{3,2,0,1:T(8,128)(2,1)S(1)}, f32[1,1024]{1,0:T(1,128)S(1)}, ...), branch_computations={%region_1.1_spmd, %region_2.9_spmd} | conditional | flops 1414399232 | bytes 54000248 | solution.py:117
  404.1 6.0 collective-permute-done
  410.1 23.2 %conditional.2 = (bf16[3,1,80,1024]{3,2,0,1:T(8,128)(2,1)}, bf16[3,1,1024]{2,0,1:T(4,128)(2,1)}) conditional(s32[]{:T(128)} %convert_element_type.96, () %tuple.75, (pred[]{:T(512)}, s32[]{:T(128)}, bf16[2,80,1024]{2,1,0:T(8,128)(2,1)}, bf16[3,1,80,1024]{3,2,0,1:T(8,128)(2,1)S(1)}, f32[1,1024]{1,0:T(1,128)S(1)}, ...), branch_computations={%region_1.1_spmd, %region_2.9_spmd} | conditional | flops 1414399232 | bytes 54000248 | solution.py:117
  434.7 5.2 collective-permute-start
  439.9 6.0 collective-permute-done
  448.6 27.0 %collective-permute-start = (bf16[3,1,80,1024]{3,2,0,1:T(8,128)(2,1)}, bf16[3,1,80,1024]{3,2,0,1:T(8,128)(2,1)S(1)}, u32[]{:S(2)}, u32[]{:S(2)}) collective-permute-start(bf16[3,1,80,1024]{3,2,0,1:T(8,128)(2,1)} %get-tuple-element.501), channel_id=1, source_target_pairs={{0,64},{64,128},{128,192},{192,256},{256,320},{320,384},{384,448},... | collective-permute-start | bytes 1474568 | tf_op jit(solution)/shard_map/while/body/eval_jaxpr/ppermute | solution.py:27
  475.6 6.1 collective-permute-done
  484.4 5.2 collective-permute-start
  489.7 6.0 collective-permute-done
  498.5 13.9 %collective-permute-start = (bf16[3,1,80,1024]{3,2,0,1:T(8,128)(2,1)}, bf16[3,1,80,1024]{3,2,0,1:T(8,128)(2,1)S(1)}, u32[]{:S(2)}, u32[]{:S(2)}) collective-permute-start(bf16[3,1,80,1024]{3,2,0,1:T(8,128)(2,1)} %get-tuple-element.501), channel_id=1, source_target_pairs={{0,64},{64,128},{128,192},{192,256},{256,320},{320,384},{384,448},... | collective-permute-start | bytes 1474568 | tf_op jit(solution)/shard_map/while/body/eval_jaxpr/ppermute | solution.py:27
  512.4 6.0 collective-permute-done
  521.2 8.7 %collective-permute-start = (bf16[3,1,80,1024]{3,2,0,1:T(8,128)(2,1)}, bf16[3,1,80,1024]{3,2,0,1:T(8,128)(2,1)S(1)}, u32[]{:S(2)}, u32[]{:S(2)}) collective-permute-start(bf16[3,1,80,1024]{3,2,0,1:T(8,128)(2,1)} %get-tuple-element.501), channel_id=1, source_target_pairs={{0,64},{64,128},{128,192},{192,256},{256,320},{320,384},{384,448},... | collective-permute-start | bytes 1474568 | tf_op jit(solution)/shard_map/while/body/eval_jaxpr/ppermute | solution.py:27
  529.9 6.0 collective-permute-done
  538.7 28.2 %collective-permute-start = (bf16[3,1,80,1024]{3,2,0,1:T(8,128)(2,1)}, bf16[3,1,80,1024]{3,2,0,1:T(8,128)(2,1)S(1)}, u32[]{:S(2)}, u32[]{:S(2)}) collective-permute-start(bf16[3,1,80,1024]{3,2,0,1:T(8,128)(2,1)} %get-tuple-element.501), channel_id=1, source_target_pairs={{0,64},{64,128},{128,192},{192,256},{256,320},{320,384},{384,448},... | collective-permute-start | bytes 1474568 | tf_op jit(solution)/shard_map/while/body/eval_jaxpr/ppermute | solution.py:27
  567.0 6.0 collective-permute-done
  576.5 74.9 %all-gather = bf16[24,2,1024]{2,1,0:T(2,128)(2,1)S(1)} all-gather(bf16[3,2,1024]{2,1,0:T(2,128)(2,1)S(1)} %copy.73), channel_id=2, replica_groups=mesh['section'=8,'dp'=64] {'section'}, dimensions={0}, use_global_device_ids=true | all-gather | bytes 110592 | tf_op jit(solution)/shard_map/all_gather | solution.py:31
  (162 shorter events, 100.0 us)
Async XLA Ops:
  7.2 646.4 %copy-start = (bf16[1024,125]{1,0:T(8,128)(2,1)S(1)}, bf16[1024,125]{1,0:T(8,128)(2,1)}, u32[]{:S(2)}) copy-start(bf16[1024,125]{1,0:T(8,128)(2,1)} %param.19) | copy-start | bytes 768004
  7.2 274.9 %all-gather.3.cloned.1.call-start = ((), (), s32[]{:S(2)}) async-start(), calls=%async_computation | async-start | bytes 8519680 | tf_op jit(solution)/shard_map/all_gather | solution.py:16
  298.4 5.3 copy-start.5
  303.7 54.0 %collective-permute-start = (bf16[3,1,80,1024]{3,2,0,1:T(8,128)(2,1)}, bf16[3,1,80,1024]{3,2,0,1:T(8,128)(2,1)S(1)}, u32[]{:S(2)}, u32[]{:S(2)}) collective-permute-start(bf16[3,1,80,1024]{3,2,0,1:T(8,128)(2,1)} %get-tuple-element.501), channel_id=1, source_target_pairs={{0,64},{64,128},{128,192},{192,256},{256,320},{320,384},{384,448},... | collective-permute-start | bytes 1474568 | tf_op jit(solution)/shard_map/while/body/eval_jaxpr/ppermute | solution.py:27
  360.4 17.2 %collective-permute-start = (bf16[3,1,80,1024]{3,2,0,1:T(8,128)(2,1)}, bf16[3,1,80,1024]{3,2,0,1:T(8,128)(2,1)S(1)}, u32[]{:S(2)}, u32[]{:S(2)}) collective-permute-start(bf16[3,1,80,1024]{3,2,0,1:T(8,128)(2,1)} %get-tuple-element.501), channel_id=1, source_target_pairs={{0,64},{64,128},{128,192},{192,256},{256,320},{320,384},{384,448},... | collective-permute-start | bytes 1474568 | tf_op jit(solution)/shard_map/while/body/eval_jaxpr/ppermute | solution.py:27
  378.8 1.9 copy-start.1
  379.0 3.8 copy-start.6
  385.9 3.7 copy-start.3
  389.6 1.9 copy-start.2
  391.5 2.0 copy-start.4
  402.2 8.0 %collective-permute-start = (bf16[3,1,80,1024]{3,2,0,1:T(8,128)(2,1)}, bf16[3,1,80,1024]{3,2,0,1:T(8,128)(2,1)S(1)}, u32[]{:S(2)}, u32[]{:S(2)}) collective-permute-start(bf16[3,1,80,1024]{3,2,0,1:T(8,128)(2,1)} %get-tuple-element.501), channel_id=1, source_target_pairs={{0,64},{64,128},{128,192},{192,256},{256,320},{320,384},{384,448},... | collective-permute-start | bytes 1474568 | tf_op jit(solution)/shard_map/while/body/eval_jaxpr/ppermute | solution.py:27
  411.3 1.9 copy-start.1
  411.5 3.8 copy-start.6
  418.4 3.7 copy-start.3
  422.1 1.9 copy-start.2
  424.0 2.0 copy-start.4
  434.7 11.2 %collective-permute-start = (bf16[3,1,80,1024]{3,2,0,1:T(8,128)(2,1)}, bf16[3,1,80,1024]{3,2,0,1:T(8,128)(2,1)S(1)}, u32[]{:S(2)}, u32[]{:S(2)}) collective-permute-start(bf16[3,1,80,1024]{3,2,0,1:T(8,128)(2,1)} %get-tuple-element.501), channel_id=1, source_target_pairs={{0,64},{64,128},{128,192},{192,256},{256,320},{320,384},{384,448},... | collective-permute-start | bytes 1474568 | tf_op jit(solution)/shard_map/while/body/eval_jaxpr/ppermute | solution.py:27
  448.6 33.1 %collective-permute-start = (bf16[3,1,80,1024]{3,2,0,1:T(8,128)(2,1)}, bf16[3,1,80,1024]{3,2,0,1:T(8,128)(2,1)S(1)}, u32[]{:S(2)}, u32[]{:S(2)}) collective-permute-start(bf16[3,1,80,1024]{3,2,0,1:T(8,128)(2,1)} %get-tuple-element.501), channel_id=1, source_target_pairs={{0,64},{64,128},{128,192},{192,256},{256,320},{320,384},{384,448},... | collective-permute-start | bytes 1474568 | tf_op jit(solution)/shard_map/while/body/eval_jaxpr/ppermute | solution.py:27
  484.4 11.3 %collective-permute-start = (bf16[3,1,80,1024]{3,2,0,1:T(8,128)(2,1)}, bf16[3,1,80,1024]{3,2,0,1:T(8,128)(2,1)S(1)}, u32[]{:S(2)}, u32[]{:S(2)}) collective-permute-start(bf16[3,1,80,1024]{3,2,0,1:T(8,128)(2,1)} %get-tuple-element.501), channel_id=1, source_target_pairs={{0,64},{64,128},{128,192},{192,256},{256,320},{320,384},{384,448},... | collective-permute-start | bytes 1474568 | tf_op jit(solution)/shard_map/while/body/eval_jaxpr/ppermute | solution.py:27
  498.5 20.0 %collective-permute-start = (bf16[3,1,80,1024]{3,2,0,1:T(8,128)(2,1)}, bf16[3,1,80,1024]{3,2,0,1:T(8,128)(2,1)S(1)}, u32[]{:S(2)}, u32[]{:S(2)}) collective-permute-start(bf16[3,1,80,1024]{3,2,0,1:T(8,128)(2,1)} %get-tuple-element.501), channel_id=1, source_target_pairs={{0,64},{64,128},{128,192},{192,256},{256,320},{320,384},{384,448},... | collective-permute-start | bytes 1474568 | tf_op jit(solution)/shard_map/while/body/eval_jaxpr/ppermute | solution.py:27
  521.2 14.8 %collective-permute-start = (bf16[3,1,80,1024]{3,2,0,1:T(8,128)(2,1)}, bf16[3,1,80,1024]{3,2,0,1:T(8,128)(2,1)S(1)}, u32[]{:S(2)}, u32[]{:S(2)}) collective-permute-start(bf16[3,1,80,1024]{3,2,0,1:T(8,128)(2,1)} %get-tuple-element.501), channel_id=1, source_target_pairs={{0,64},{64,128},{128,192},{192,256},{256,320},{320,384},{384,448},... | collective-permute-start | bytes 1474568 | tf_op jit(solution)/shard_map/while/body/eval_jaxpr/ppermute | solution.py:27
  538.7 34.3 %collective-permute-start = (bf16[3,1,80,1024]{3,2,0,1:T(8,128)(2,1)}, bf16[3,1,80,1024]{3,2,0,1:T(8,128)(2,1)S(1)}, u32[]{:S(2)}, u32[]{:S(2)}) collective-permute-start(bf16[3,1,80,1024]{3,2,0,1:T(8,128)(2,1)} %get-tuple-element.501), channel_id=1, source_target_pairs={{0,64},{64,128},{128,192},{192,256},{256,320},{320,384},{384,448},... | collective-permute-start | bytes 1474568 | tf_op jit(solution)/shard_map/while/body/eval_jaxpr/ppermute | solution.py:27
Sparse Core Ops, SparseCore 0:
  10.5 271.5 all-gather.2
where the time goes:
time: 664 us; the launch traced here: 662 us
  waiting for transfers between devices  332 us (50%)
  starting transfers between devices  143 us (22%)
  blocking collectives  74.9 us (11%)
  local copies, waits for them, and re-layouts  48.8 us (7%)
  matrix products  24.3 us (4%)
  other arithmetic  23.5 us (4%)
  between operations  14.1 us (2%)
    all_gather x1, waiting for transfers between devices, gather_turned(): lax.all_gather(both, axis, axis=0, tiled=True)  272 us
    ppermute x9, starting transfers between devices, passed_along(): return lax.ppermute(block, axis, route)  143 us
    all_gather x1, blocking collectives, picked(): lax.all_gather(shard, axis)  74.9 us
    ppermute x9, waiting for transfers between devices, passed_along(): return lax.ppermute(block, axis, route)  60.5 us
    dot_general x19, matrix products, contract(): return jnp.einsum(spec, left, right, preferred_element_type=jnp.float32)  22.4 us
  transfers between devices with their start and end apart: 10, of which 10 were waited for; matrix products, arithmetic and copies ran while one was open for 0% of the time, Pallas kernels for 0%

commit v1 on v0

--- a/solution.py
+++ b/solution.py
@@ -13,7 +13,13 @@
 def gather_turned(arrays, axis, dims):
     turned = [jnp.moveaxis(a, dim, 0) for a, dim in zip(arrays, dims)]
     both = jnp.concatenate([t.reshape(len(t), -1) for t in turned], axis=1)
-    result, at, gathered = (lax.all_gather(both, axis, axis=0, tiled=True), 0, [])
+    result, at, gathered = (
+        jnp.concatenate(
+            lax.all_to_all(jnp.stack([both] * lax.axis_size(axis)), axis, 0, 0), axis=0
+        ),
+        0,
+        [],
+    )
     for t, dim in zip(turned, dims):
         share = result[:, at : at + t[0].size].reshape(-1, *t.shape[1:])
         gathered.append(jnp.moveaxis(share, 0, dim))

time: 664 us -> 533 us (0.80)
  the two profiles are of different devices: /device:TPU:5 before, /device:TPU:69 now
where the time goes in v1:
time: 533 us; the launch traced here: 531 us
  waiting for transfers between devices  247 us (46%)
  starting transfers between devices  109 us (20%)
  blocking collectives  73.5 us (14%)
  local copies, waits for them, and re-layouts  53.1 us (10%)
  matrix products  24.4 us (5%)
  other arithmetic  22.9 us (4%)
    all_to_all x1, waiting for transfers between devices, gather_turned(): lax.all_to_all(jnp.stack([both] * lax.axis_size(axis)), axis, 0, 0)  183 us
    ppermute x9, starting transfers between devices, passed_along(): return lax.ppermute(block, axis, route)  97.6 us
    all_gather x1, blocking collectives, picked(): lax.all_gather(shard, axis)  73.5 us
    ppermute x9, waiting for transfers between devices, passed_along(): return lax.ppermute(block, axis, route)  64.3 us
    dot_general x19, matrix products, contract(): return jnp.einsum(spec, left, right, preferred_element_type=jnp.float32)  22.4 us
    another operation x22, local copies, waits for them, and re-layouts  12.1 us
    dynamic_update_slice x9, other arithmetic, advance(): collected = lax.dynamic_update_slice_in_dim(collected, update, slot_clip, 1)  11.7 us
    all_to_all x1, starting transfers between devices, gather_turned(): lax.all_to_all(jnp.stack([both] * lax.axis_size(axis)), axis, 0, 0)  11.2 us
  transfers between devices with their start and end apart: 10, of which 10 were waited for; matrix products, arithmetic and copies ran while one was open for 0% of the time, Pallas kernels for 0%

profile of v1, /device:TPU:69, one launch (start us, length us, event | category | flops | bytes accessed | tf_op | source)
XLA Modules:
  0.0 530.9 jit_solution(3454206021531455515)
XLA Ops:
  7.4 11.2 %all-to-all-start = ((bf16[64,16,4096]{2,1,0:T(8,128)(2,1)}), bf16[64,16,4096]{2,1,0:T(8,128)(2,1)}, u32[]{:S(2)}, u32[]{:S(2)}) async-start(bf16[64,16,4096]{2,1,0:T(8,128)(2,1)} %stack.2), calls=%async_computation | async-start | bytes 16777216 | tf_op jit(solution)/shard_map/all_to_all | solution.py:18
  18.6 182.6 %all-to-all-done = bf16[64,16,4096]{2,1,0:T(8,128)(2,1)} async-done(((bf16[64,16,4096]{2,1,0:T(8,128)(2,1)}), bf16[64,16,4096]{2,1,0:T(8,128)(2,1)}, u32[]{:S(2)}, u32[]{:S(2)}) %all-to-all-start) | async-done | bytes 8388640 | tf_op jit(solution)/shard_map/all_to_all | solution.py:18
  201.2 4.7 fusion.96
  222.7 230.4 %while.16 = (s32[]{:T(128)}, bf16[3,1,80,1024]{3,2,0,1:T(8,128)(2,1)}, bf16[3,2,1024]{2,0,1:T(4,128)(2,1)}, s32[]{:T(128)}, pred[]{:T(512)}, /*index=5*/bf16[2,8...) while((s32[]{:T(128)}, ...), condition=%wide.region_10.11_spmd, body=%wide.region_0.10_spmd.sunk | while | flops 1414402304 | bytes 55991232 | solution.py:135
  222.7 9.7 %collective-permute-start = (bf16[3,1,80,1024]{3,2,0,1:T(8,128)(2,1)}, bf16[3,1,80,1024]{3,2,0,1:T(8,128)(2,1)S(1)}, u32[]{:S(2)}, u32[]{:S(2)}) collective-permute-start(bf16[3,1,80,1024]{3,2,0,1:T(8,128)(2,1)} %get-tuple-element.501), channel_id=1, source_target_pairs={{0,64},{64,128},{128,192},{192,256},{256,320},{320,384},{384,448},... | collective-permute-start | bytes 1474568 | tf_op jit(solution)/shard_map/while/body/eval_jaxpr/ppermute | solution.py:33
  232.5 11.3 %collective-permute-done = bf16[3,1,80,1024]{3,2,0,1:T(8,128)(2,1)S(1)} collective-permute-done((bf16[3,1,80,1024]{3,2,0,1:T(8,128)(2,1)}, bf16[3,1,80,1024]{3,2,0,1:T(8,128)(2,1)S(1)}, u32[]{:S(2)}, u32[]{:S(2)}) %collective-permute-start) | collective-permute-done | bytes 491552 | tf_op jit(solution)/shard_map/while/body/eval_jaxpr/ppermute | solution.py:33
  246.5 5.2 collective-permute-start
  251.8 6.1 %collective-permute-done = bf16[3,1,80,1024]{3,2,0,1:T(8,128)(2,1)S(1)} collective-permute-done((bf16[3,1,80,1024]{3,2,0,1:T(8,128)(2,1)}, bf16[3,1,80,1024]{3,2,0,1:T(8,128)(2,1)S(1)}, u32[]{:S(2)}, u32[]{:S(2)}) %collective-permute-start) | collective-permute-done | bytes 491552 | tf_op jit(solution)/shard_map/while/body/eval_jaxpr/ppermute | solution.py:33
  257.9 23.3 %conditional.2 = (bf16[3,1,80,1024]{3,2,0,1:T(8,128)(2,1)}, bf16[3,1,1024]{2,0,1:T(4,128)(2,1)}) conditional(s32[]{:T(128)} %convert_element_type.96, () %tuple.75, (pred[]{:T(512)}, s32[]{:T(128)}, bf16[2,80,1024]{2,1,0:T(8,128)(2,1)}, bf16[3,1,80,1024]{3,2,0,1:T(8,128)(2,1)S(1)}, f32[1,1024]{1,0:T(1,128)S(1)}, ...), branch_computations={%region_1.1_spmd, %region_2.9_spmd} | conditional | flops 1414399232 | bytes 54000248 | solution.py:123
  284.4 10.6 %collective-permute-done = bf16[3,1,80,1024]{3,2,0,1:T(8,128)(2,1)S(1)} collective-permute-done((bf16[3,1,80,1024]{3,2,0,1:T(8,128)(2,1)}, bf16[3,1,80,1024]{3,2,0,1:T(8,128)(2,1)S(1)}, u32[]{:S(2)}, u32[]{:S(2)}) %collective-permute-start) | collective-permute-done | bytes 491552 | tf_op jit(solution)/shard_map/while/body/eval_jaxpr/ppermute | solution.py:33
  294.9 23.2 %conditional.2 = (bf16[3,1,80,1024]{3,2,0,1:T(8,128)(2,1)}, bf16[3,1,1024]{2,0,1:T(4,128)(2,1)}) conditional(s32[]{:T(128)} %convert_element_type.96, () %tuple.75, (pred[]{:T(512)}, s32[]{:T(128)}, bf16[2,80,1024]{2,1,0:T(8,128)(2,1)}, bf16[3,1,80,1024]{3,2,0,1:T(8,128)(2,1)S(1)}, f32[1,1024]{1,0:T(1,128)S(1)}, ...), branch_computations={%region_1.1_spmd, %region_2.9_spmd} | conditional | flops 1414399232 | bytes 54000248 | solution.py:123
  319.5 5.2 collective-permute-start
  324.7 6.0 %collective-permute-done = bf16[3,1,80,1024]{3,2,0,1:T(8,128)(2,1)S(1)} collective-permute-done((bf16[3,1,80,1024]{3,2,0,1:T(8,128)(2,1)}, bf16[3,1,80,1024]{3,2,0,1:T(8,128)(2,1)S(1)}, u32[]{:S(2)}, u32[]{:S(2)}) %collective-permute-start) | collective-permute-done | bytes 491552 | tf_op jit(solution)/shard_map/while/body/eval_jaxpr/ppermute | solution.py:33
  333.5 27.0 %collective-permute-start = (bf16[3,1,80,1024]{3,2,0,1:T(8,128)(2,1)}, bf16[3,1,80,1024]{3,2,0,1:T(8,128)(2,1)S(1)}, u32[]{:S(2)}, u32[]{:S(2)}) collective-permute-start(bf16[3,1,80,1024]{3,2,0,1:T(8,128)(2,1)} %get-tuple-element.501), channel_id=1, source_target_pairs={{0,64},{64,128},{128,192},{192,256},{256,320},{320,384},{384,448},... | collective-permute-start | bytes 1474568 | tf_op jit(solution)/shard_map/while/body/eval_jaxpr/ppermute | solution.py:33
  360.5 6.0 %collective-permute-done = bf16[3,1,80,1024]{3,2,0,1:T(8,128)(2,1)S(1)} collective-permute-done((bf16[3,1,80,1024]{3,2,0,1:T(8,128)(2,1)}, bf16[3,1,80,1024]{3,2,0,1:T(8,128)(2,1)S(1)}, u32[]{:S(2)}, u32[]{:S(2)}) %collective-permute-start) | collective-permute-done | bytes 491552 | tf_op jit(solution)/shard_map/while/body/eval_jaxpr/ppermute | solution.py:33
  369.3 5.2 collective-permute-start
  374.5 6.0 %collective-permute-done = bf16[3,1,80,1024]{3,2,0,1:T(8,128)(2,1)S(1)} collective-permute-done((bf16[3,1,80,1024]{3,2,0,1:T(8,128)(2,1)}, bf16[3,1,80,1024]{3,2,0,1:T(8,128)(2,1)S(1)}, u32[]{:S(2)}, u32[]{:S(2)}) %collective-permute-start) | collective-permute-done | bytes 491552 | tf_op jit(solution)/shard_map/while/body/eval_jaxpr/ppermute | solution.py:33
  383.3 12.0 %collective-permute-start = (bf16[3,1,80,1024]{3,2,0,1:T(8,128)(2,1)}, bf16[3,1,80,1024]{3,2,0,1:T(8,128)(2,1)S(1)}, u32[]{:S(2)}, u32[]{:S(2)}) collective-permute-start(bf16[3,1,80,1024]{3,2,0,1:T(8,128)(2,1)} %get-tuple-element.501), channel_id=1, source_target_pairs={{0,64},{64,128},{128,192},{192,256},{256,320},{320,384},{384,448},... | collective-permute-start | bytes 1474568 | tf_op jit(solution)/shard_map/while/body/eval_jaxpr/ppermute | solution.py:33
  395.4 6.0 %collective-permute-done = bf16[3,1,80,1024]{3,2,0,1:T(8,128)(2,1)S(1)} collective-permute-done((bf16[3,1,80,1024]{3,2,0,1:T(8,128)(2,1)}, bf16[3,1,80,1024]{3,2,0,1:T(8,128)(2,1)S(1)}, u32[]{:S(2)}, u32[]{:S(2)}) %collective-permute-start) | collective-permute-done | bytes 491552 | tf_op jit(solution)/shard_map/while/body/eval_jaxpr/ppermute | solution.py:33
  404.2 5.2 collective-permute-start
  409.4 6.0 %collective-permute-done = bf16[3,1,80,1024]{3,2,0,1:T(8,128)(2,1)S(1)} collective-permute-done((bf16[3,1,80,1024]{3,2,0,1:T(8,128)(2,1)}, bf16[3,1,80,1024]{3,2,0,1:T(8,128)(2,1)S(1)}, u32[]{:S(2)}, u32[]{:S(2)}) %collective-permute-start) | collective-permute-done | bytes 491552 | tf_op jit(solution)/shard_map/while/body/eval_jaxpr/ppermute | solution.py:33
  418.1 26.1 %collective-permute-start = (bf16[3,1,80,1024]{3,2,0,1:T(8,128)(2,1)}, bf16[3,1,80,1024]{3,2,0,1:T(8,128)(2,1)S(1)}, u32[]{:S(2)}, u32[]{:S(2)}) collective-permute-start(bf16[3,1,80,1024]{3,2,0,1:T(8,128)(2,1)} %get-tuple-element.501), channel_id=1, source_target_pairs={{0,64},{64,128},{128,192},{192,256},{256,320},{320,384},{384,448},... | collective-permute-start | bytes 1474568 | tf_op jit(solution)/shard_map/while/body/eval_jaxpr/ppermute | solution.py:33
  444.3 6.0 %collective-permute-done = bf16[3,1,80,1024]{3,2,0,1:T(8,128)(2,1)S(1)} collective-permute-done((bf16[3,1,80,1024]{3,2,0,1:T(8,128)(2,1)}, bf16[3,1,80,1024]{3,2,0,1:T(8,128)(2,1)S(1)}, u32[]{:S(2)}, u32[]{:S(2)}) %collective-permute-start) | collective-permute-done | bytes 491552 | tf_op jit(solution)/shard_map/while/body/eval_jaxpr/ppermute | solution.py:33
  453.8 73.5 %all-gather = bf16[24,2,1024]{2,1,0:T(2,128)(2,1)S(1)} all-gather(bf16[3,2,1024]{2,1,0:T(2,128)(2,1)S(1)} %copy.69), channel_id=2, replica_groups=mesh['section'=8,'dp'=64] {'section'}, dimensions={0}, use_global_device_ids=true | all-gather | bytes 110592 | tf_op jit(solution)/shard_map/all_gather | solution.py:37
  (162 shorter events, 107.6 us)
Async XLA Ops:
  0.6 529.0 %copy-start = (bf16[1024,125]{1,0:T(8,128)(2,1)S(1)}, bf16[1024,125]{1,0:T(8,128)(2,1)}, u32[]{:S(2)}) copy-start(bf16[1024,125]{1,0:T(8,128)(2,1)} %param.19) | copy-start | bytes 768004
  7.4 193.8 %all-to-all-start = ((bf16[64,16,4096]{2,1,0:T(8,128)(2,1)}), bf16[64,16,4096]{2,1,0:T(8,128)(2,1)}, u32[]{:S(2)}, u32[]{:S(2)}) async-start(bf16[64,16,4096]{2,1,0:T(8,128)(2,1)} %stack.2), calls=%async_computation | async-start | bytes 16777216 | tf_op jit(solution)/shard_map/all_to_all | solution.py:18
  220.0 2.8 copy-start.5
  222.7 21.1 %collective-permute-start = (bf16[3,1,80,1024]{3,2,0,1:T(8,128)(2,1)}, bf16[3,1,80,1024]{3,2,0,1:T(8,128)(2,1)S(1)}, u32[]{:S(2)}, u32[]{:S(2)}) collective-permute-start(bf16[3,1,80,1024]{3,2,0,1:T(8,128)(2,1)} %get-tuple-element.501), channel_id=1, source_target_pairs={{0,64},{64,128},{128,192},{192,256},{256,320},{320,384},{384,448},... | collective-permute-start | bytes 1474568 | tf_op jit(solution)/shard_map/while/body/eval_jaxpr/ppermute | solution.py:33
  246.5 11.3 %collective-permute-start = (bf16[3,1,80,1024]{3,2,0,1:T(8,128)(2,1)}, bf16[3,1,80,1024]{3,2,0,1:T(8,128)(2,1)S(1)}, u32[]{:S(2)}, u32[]{:S(2)}) collective-permute-start(bf16[3,1,80,1024]{3,2,0,1:T(8,128)(2,1)} %get-tuple-element.501), channel_id=1, source_target_pairs={{0,64},{64,128},{128,192},{192,256},{256,320},{320,384},{384,448},... | collective-permute-start | bytes 1474568 | tf_op jit(solution)/shard_map/while/body/eval_jaxpr/ppermute | solution.py:33
  259.0 1.9 copy-start.1
  259.2 3.8 copy-start.6
  266.1 3.7 copy-start.3
  269.9 1.9 copy-start.2
  271.7 2.0 copy-start.4
  282.4 12.5 %collective-permute-start = (bf16[3,1,80,1024]{3,2,0,1:T(8,128)(2,1)}, bf16[3,1,80,1024]{3,2,0,1:T(8,128)(2,1)S(1)}, u32[]{:S(2)}, u32[]{:S(2)}) collective-permute-start(bf16[3,1,80,1024]{3,2,0,1:T(8,128)(2,1)} %get-tuple-element.501), channel_id=1, source_target_pairs={{0,64},{64,128},{128,192},{192,256},{256,320},{320,384},{384,448},... | collective-permute-start | bytes 1474568 | tf_op jit(solution)/shard_map/while/body/eval_jaxpr/ppermute | solution.py:33
  296.1 1.9 copy-start.1
  296.3 3.8 copy-start.6
  303.2 3.7 copy-start.3
  306.9 1.9 copy-start.2
  308.8 2.0 copy-start.4
  319.5 11.3 %collective-permute-start = (bf16[3,1,80,1024]{3,2,0,1:T(8,128)(2,1)}, bf16[3,1,80,1024]{3,2,0,1:T(8,128)(2,1)S(1)}, u32[]{:S(2)}, u32[]{:S(2)}) collective-permute-start(bf16[3,1,80,1024]{3,2,0,1:T(8,128)(2,1)} %get-tuple-element.501), channel_id=1, source_target_pairs={{0,64},{64,128},{128,192},{192,256},{256,320},{320,384},{384,448},... | collective-permute-start | bytes 1474568 | tf_op jit(solution)/shard_map/while/body/eval_jaxpr/ppermute | solution.py:33
  333.5 33.1 %collective-permute-start = (bf16[3,1,80,1024]{3,2,0,1:T(8,128)(2,1)}, bf16[3,1,80,1024]{3,2,0,1:T(8,128)(2,1)S(1)}, u32[]{:S(2)}, u32[]{:S(2)}) collective-permute-start(bf16[3,1,80,1024]{3,2,0,1:T(8,128)(2,1)} %get-tuple-element.501), channel_id=1, source_target_pairs={{0,64},{64,128},{128,192},{192,256},{256,320},{320,384},{384,448},... | collective-permute-start | bytes 1474568 | tf_op jit(solution)/shard_map/while/body/eval_jaxpr/ppermute | solution.py:33
  369.3 11.2 %collective-permute-start = (bf16[3,1,80,1024]{3,2,0,1:T(8,128)(2,1)}, bf16[3,1,80,1024]{3,2,0,1:T(8,128)(2,1)S(1)}, u32[]{:S(2)}, u32[]{:S(2)}) collective-permute-start(bf16[3,1,80,1024]{3,2,0,1:T(8,128)(2,1)} %get-tuple-element.501), channel_id=1, source_target_pairs={{0,64},{64,128},{128,192},{192,256},{256,320},{320,384},{384,448},... | collective-permute-start | bytes 1474568 | tf_op jit(solution)/shard_map/while/body/eval_jaxpr/ppermute | solution.py:33
  383.3 18.1 %collective-permute-start = (bf16[3,1,80,1024]{3,2,0,1:T(8,128)(2,1)}, bf16[3,1,80,1024]{3,2,0,1:T(8,128)(2,1)S(1)}, u32[]{:S(2)}, u32[]{:S(2)}) collective-permute-start(bf16[3,1,80,1024]{3,2,0,1:T(8,128)(2,1)} %get-tuple-element.501), channel_id=1, source_target_pairs={{0,64},{64,128},{128,192},{192,256},{256,320},{320,384},{384,448},... | collective-permute-start | bytes 1474568 | tf_op jit(solution)/shard_map/while/body/eval_jaxpr/ppermute | solution.py:33
  404.2 11.2 %collective-permute-start = (bf16[3,1,80,1024]{3,2,0,1:T(8,128)(2,1)}, bf16[3,1,80,1024]{3,2,0,1:T(8,128)(2,1)S(1)}, u32[]{:S(2)}, u32[]{:S(2)}) collective-permute-start(bf16[3,1,80,1024]{3,2,0,1:T(8,128)(2,1)} %get-tuple-element.501), channel_id=1, source_target_pairs={{0,64},{64,128},{128,192},{192,256},{256,320},{320,384},{384,448},... | collective-permute-start | bytes 1474568 | tf_op jit(solution)/shard_map/while/body/eval_jaxpr/ppermute | solution.py:33
  418.1 32.2 %collective-permute-start = (bf16[3,1,80,1024]{3,2,0,1:T(8,128)(2,1)}, bf16[3,1,80,1024]{3,2,0,1:T(8,128)(2,1)S(1)}, u32[]{:S(2)}, u32[]{:S(2)}) collective-permute-start(bf16[3,1,80,1024]{3,2,0,1:T(8,128)(2,1)} %get-tuple-element.501), channel_id=1, source_target_pairs={{0,64},{64,128},{128,192},{192,256},{256,320},{320,384},{384,448},... | collective-permute-start | bytes 1474568 | tf_op jit(solution)/shard_map/while/body/eval_jaxpr/ppermute | solution.py:33
